TPU v7x, 128 devices: a whole 4x4x4 slice. The times are simulated.
128 devices in a mesh: col: 16 (over z, x), row: 8 (over y, core).
Axes of the slice: x: 4, y: 4, z: 4, core: 2. Of those that a mesh axis runs over, the one named last changes fastest.
Arguments:
- parent_front: float32 [12288, 12288], P('row', 'col'), as said below
- child_blocks: float32 [8192, 16384], P('row', 'col'), as said below
- child_map: int32 [2, 64], replicated, may hold values from 0 to 95, as said below
- child_order: int32 [2], replicated, may hold values from 4096 to 8192, as said below
Outputs:
- factored: float32 [12288, 12288], P('row', 'col')
Inputs may be any that keep to these rules, and one draw needn't show every extreme that they name: parent_front is symmetric. `child_blocks`: each child's block, in true tile order, is symmetric. `child_map`: along each child's 64 tiles the parent tile numbers rise strictly. `child_order`: one child has exactly 8192; every child has at least 4096.
All inputs are finite; a program needn't handle non-finite values.
Results may differ from a plain program's by a relative error of at most 0.0001.
Values sent between devices are 32-bit elements; how exact they have to be, the bound alone decides.
A program may use at most 128 MiB of HBM per device.

v0:
```python
import jax
import jax.numpy as jnp
from jax import lax
from jax.sharding import PartitionSpec as P

B = 128
NPIV = 256
HIGHEST_PRECISION = lax.Precision.HIGHEST


def broadcast(value, axis, source):
    kept = jnp.where(lax.axis_index(axis) == source, value, 0).astype(value.dtype)
    return lax.psum(kept, axis)


def plan_slots(targets, usable, block_size, dest_count, slot_count):
    item_total = targets.shape[0]
    places = jnp.arange(item_total, dtype=jnp.int32)
    owners = targets // block_size
    within = targets % block_size
    earlier = (
        (owners[:, None] == owners[None, :]) & usable[None, :] & (places[None, :] < places[:, None])
    )
    ranking = jnp.sum(earlier.astype(jnp.int32), axis=1)
    picked = (
        usable[None, None, :]
        & (owners[None, None, :] == jnp.arange(dest_count, dtype=jnp.int32)[:, None, None])
        & (ranking[None, None, :] == jnp.arange(slot_count, dtype=jnp.int32)[None, :, None])
    )
    filled = jnp.any(picked, axis=2)
    source = jnp.sum(jnp.where(picked, places[None, None, :], 0), axis=2)
    labels = jnp.where(filled, jnp.sum(jnp.where(picked, within[None, None, :], 0), axis=2), -1)
    return (source, filled, labels)


def child_targets(child_map, child_order, child_index, tile_numbers):
    chosen = jnp.arange(child_map.shape[0], dtype=jnp.int32) == child_index
    row_map = jnp.sum(jnp.where(chosen[:, None], child_map, 0), axis=0)
    order_limit = jnp.sum(jnp.where(chosen, child_order, 0))
    onehot = tile_numbers[:, None] == jnp.arange(row_map.shape[0], dtype=jnp.int32)[None, :]
    targets = jnp.sum(jnp.where(onehot, row_map[None, :], 0), axis=1)
    return (targets, tile_numbers * B < order_limit)


def shards(parent_front, child_blocks, child_map, child_order):
    rows_grid = lax.axis_size("row")
    cols_grid = lax.axis_size("col")
    row_index = lax.axis_index("row")
    col_index = lax.axis_index("col")
    local_rows, local_cols = parent_front.shape
    kid_rows, kid_cols = child_blocks.shape
    kid_count = child_map.shape[0]
    per_child = cols_grid // kid_count
    my_child = col_index // per_child
    my_slot = col_index % per_child
    tiles_down = kid_rows // B
    tiles_across = kid_cols // B
    parent_rtiles = local_rows // B
    parent_ctiles = local_cols // B
    cap_rows = (parent_rtiles + rows_grid - 1) // rows_grid
    cap_cols = (parent_ctiles + per_child - 1) // per_child
    row_tiles = jnp.arange(tiles_down, dtype=jnp.int32) * rows_grid + row_index
    col_tiles = jnp.arange(tiles_across, dtype=jnp.int32) * per_child + my_slot
    chosen = jnp.arange(kid_count, dtype=jnp.int32) == my_child
    order_limit = jnp.sum(jnp.where(chosen, child_order, 0))
    within = jnp.arange(B, dtype=jnp.int32)
    row_alive = (row_tiles[:, None] * B + within[None, :]).reshape(-1) < order_limit
    col_alive = (col_tiles[:, None] * B + within[None, :]).reshape(-1) < order_limit
    children = jnp.where(row_alive[:, None] & col_alive[None, :], child_blocks, 0.0)
    col_targets, col_usable = child_targets(child_map, child_order, my_child, col_tiles)
    row_targets, row_usable = child_targets(child_map, child_order, my_child, row_tiles)
    source, filled, labels = plan_slots(row_targets, row_usable, parent_rtiles, rows_grid, cap_rows)
    row_tiled = children.reshape(tiles_down, B, kid_cols)
    outgoing = jnp.where(filled[:, :, None, None], row_tiled[source], 0.0)
    arrived, arrived_labels = (
        lax.all_to_all(outgoing, "row", split_axis=0, concat_axis=0, tiled=True),
        lax.all_to_all(labels, "row", split_axis=0, concat_axis=0, tiled=True),
    )
    flat_labels = arrived_labels.reshape(-1)
    flat_tiles = arrived.reshape(-1, B, kid_cols)
    slots_here = flat_labels.shape[0]
    matches = flat_labels[None, :] == jnp.arange(parent_rtiles, dtype=jnp.int32)[:, None]
    present = jnp.any(matches, axis=1)
    pick_slot = jnp.sum(
        jnp.where(matches, jnp.arange(slots_here, dtype=jnp.int32)[None, :], 0), axis=1
    )
    framed = jnp.where(present[:, None, None], flat_tiles[pick_slot], 0.0).reshape(
        local_rows, kid_cols
    )
    col_source, col_filled, col_labels = plan_slots(
        col_targets, col_usable, parent_ctiles, cols_grid, cap_cols
    )
    columns = framed.reshape(local_rows, tiles_across, B)
    outgoing_cols = jnp.where(col_filled[None, :, :, None], columns[:, col_source], 0.0)
    arrived_cols, labels_back = (
        lax.all_to_all(outgoing_cols, "col", split_axis=1, concat_axis=1, tiled=True),
        lax.all_to_all(col_labels[None], "col", split_axis=1, concat_axis=1, tiled=True),
    )
    landing = (
        labels_back.reshape(-1)[:, None] == jnp.arange(parent_ctiles, dtype=jnp.int32)[None, :]
    ).astype(jnp.float32)
    assembled = jnp.einsum(
        "rsb,su->rub",
        arrived_cols.reshape(local_rows, -1, B),
        landing,
        precision=HIGHEST_PRECISION,
        preferred_element_type=jnp.float32,
    ).reshape(local_rows, local_cols)
    front_local = parent_front + assembled
    panel_width = B
    step_count = NPIV // panel_width
    global_rows = row_index * local_rows + jnp.arange(local_rows, dtype=jnp.int32)
    global_cols = col_index * local_cols + jnp.arange(local_cols, dtype=jnp.int32)
    zero_index = jnp.int32(0)

    def fetch_panel(piece_cols, panel_start):
        return broadcast(piece_cols, "col", panel_start // local_cols)

    def finish(raw_panel, panel_start):
        holder = panel_start // local_rows
        offset = panel_start % local_rows
        corner = lax.dynamic_slice(raw_panel, (offset, zero_index), (panel_width, panel_width))
        corner = broadcast(corner, "row", holder)
        factor = jnp.linalg.cholesky(corner)
        solved = lax.linalg.triangular_solve(
            factor, raw_panel, left_side=False, lower=True, transpose_a=True
        )
        placed = lax.dynamic_update_slice(
            solved, factor, (panel_start - row_index * local_rows, zero_index)
        )
        in_corner = (global_rows >= panel_start) & (global_rows < panel_start + panel_width)
        left_rows = jnp.where(
            global_rows[:, None] < panel_start, 0.0, jnp.where(in_corner[:, None], placed, solved)
        )
        col_base = col_index * local_cols
        sender = col_base // local_rows
        part_rows = lax.dynamic_slice(
            left_rows, (col_base % local_rows, zero_index), (local_cols, panel_width)
        )
        across = broadcast(part_rows, "row", sender)
        return (left_rows, across)

    def apply_update(front_now, left_rows, across, panel_start):
        panel_end = panel_start + panel_width
        trailing = (global_rows[:, None] >= panel_end) & (global_cols[None, :] >= panel_end)
        product = lax.dot_general(
            left_rows,
            across,
            (((1,), (1,)), ((), ())),
            precision=HIGHEST_PRECISION,
            preferred_element_type=jnp.float32,
        )
        front_now = jnp.where(trailing, front_now - product, front_now)
        written = lax.dynamic_update_slice(
            front_now, left_rows, (zero_index, panel_start % local_cols)
        )
        in_panel = (global_cols >= panel_start) & (global_cols < panel_end)
        return jnp.where(in_panel[None, :], written, front_now)

    def advance_plain(step_number, front_now):
        panel_start = step_number * panel_width
        raw_panel = fetch_panel(
            lax.dynamic_slice(
                front_now, (zero_index, panel_start % local_cols), (local_rows, panel_width)
            ),
            panel_start,
        )
        left_rows, across = finish(raw_panel, panel_start)
        return apply_update(front_now, left_rows, across, panel_start)

    front_local = lax.fori_loop(0, step_count, advance_plain, front_local)
    upper_part = (global_rows[:, None] < NPIV) & (global_cols[None, :] >= NPIV)
    return jnp.where(upper_part, 0.0, front_local)


def solution(mesh):
    placed = (P("row", "col"), P("row", "col"), P(), P())
    return jax.shard_map(
        shards, mesh=mesh, in_specs=placed, out_specs=P("row", "col"), check_vma=False
    )
```

profile of v0, /device:TPU:0, one launch (start us, length us, event | category | flops | bytes accessed | tf_op | source)
XLA Modules:
  0.0 922.4 jit_solution(13344825785148846199)
XLA Ops:
  17.0 4.7 and_select_fusion.1
  21.7 6.5 gather_fusion
  28.1 8.6 broadcast_select_fusion.1
  36.8 5.0 all-to-all-start.2
  44.4 92.0 %all-to-all-done.2 = f32[8,2,128,1024]{3,2,1,0:T(8,128)} async-done(((f32[8,2,128,1024]{3,2,1,0:T(8,128)}), f32[8,2,128,1024]{3,2,1,0:T(8,128)}, u32[]{:S(2)}, u32[]{:S(2)}) %all-to-all-start.2) | async-done | bytes 8388640 | tf_op jit(solution)/shard_map/all_to_all | solution.py:76
  136.4 7.9 all-to-all-start
  144.3 7.0 gather_fusion.1
  159.1 8.6 gather_fusion.2
  167.7 10.4 %fusion.13 = f32[1536,16,1,128]{3,0,2,1:T(8,128)} fusion(f32[16,1536,128]{2,1,0:T(8,128)} %gather_fusion.2, pred[16]{0:T(512)(128)(4,1)S(1)} %fusion.32), kind=kLoop, calls=%fused_computation.32 | loop fusion | flops 3145728 | bytes 25165840 | tf_op jit(solution)/shard_map/jit(_where)/select_n | solution.py:94
  178.1 7.3 all-to-all-start.3
  185.4 6.0 copy.57
  191.8 176.9 %all-to-all-done.3 = f32[1536,16,1,128]{3,0,2,1:T(8,128)} async-done(((f32[1536,16,1,128]{3,0,2,1:T(8,128)}), f32[1536,16,1,128]{3,0,2,1:T(8,128)}, u32[]{:S(2)}, u32[]{:S(2)}) %all-to-all-start.3) | async-done | bytes 12582944 | tf_op jit(solution)/shard_map/all_to_all | solution.py:96
  368.8 19.7 %fusion.17 = f32[1536,6,128]{2,1,0:T(8,128)} fusion(f32[1536,16,1,128]{3,0,2,1:T(8,128)} %all-to-all-done.3, s32[16]{0:T(128)S(1)} %reduce.25), kind=kOutput, calls=%fused_computation.41 | convolution fusion | flops 226492512 | bytes 17301568 | tf_op jit(solution)/shard_map/rsb,su->rub/dot_general | solution.py:102
  388.4 6.0 copy.56
  394.5 6.9 bitcast_add_fusion.1
  401.4 6.0 copy.58
  407.4 503.0 %while.18 = (s32[]{:T(128)}, f32[1536,768]{1,0:T(8,128)}, s32[]{:T(128)}, s32[]{:T(128)}, s32[]{:T(128)}, /*index=5*/s32[]{:T(128)}, s32[]{:T(128)}, s32[]{:T(12...) while((s32[]{:T(128)}, f32[1536,768]{1,0:T(8,128)}, ...), condition=%wide.region_20.21_spmd.clone.clone, body=%wide.region_14.20_spmd.clone.clone.sunk | while | flops 2118905600 | bytes 28462080 | solution.py:171
  410.2 86.2 %all-reduce.4.cloned.1.call-done = f32[1536,128]{1,0:T(8,128)} async-done(((f32[1536,128]{1,0:T(8,128)}), f32[1536,128]{1,0:T(8,128)}) %all-reduce.4.cloned.1.call-update) | async-done | bytes 786448 | tf_op jit(solution)/shard_map/while/body/eval_jaxpr/psum | solution.py:13
  498.1 58.8 %all-reduce.6.cloned.1.call-done = f32[128,128]{1,0:T(8,128)} async-done(((f32[128,128]{1,0:T(8,128)}), f32[128,128]{1,0:T(8,128)}) %all-reduce.6.cloned.1.call-update) | async-done | bytes 65552 | tf_op jit(solution)/shard_map/while/body/eval_jaxpr/psum | solution.py:13
  558.6 11.7 %cholesky.80 = f32[128,128]{1,0:T(8,128)S(1)} custom-call(f32[128,128]{1,0:T(8,128)S(1)} %fusion.54), custom_call_target="Cholesky" | custom-call | tf_op jit(solution)/shard_map/while/body/eval_jaxpr/jit(cholesky)/cholesky | solution.py:124
  571.7 9.8 %custom-call.31 = f32[1,128,128]{1,2,0:T(8,128)S(1)} custom-call(f32[1,128,128]{2,1,0:T(8,128)S(1)} %select_bitcast_fusion.4), custom_call_target="InvertDiagBlocksLowerTriangular" | custom-call | tf_op jit(solution)/shard_map/while/body/eval_jaxpr/triangular_solve | solution.py:125
  585.4 59.4 %all-reduce.8.cloned.1.call-done = f32[768,128]{1,0:T(8,128)} async-done(((f32[768,128]{1,0:T(8,128)}), f32[768,128]{1,0:T(8,128)}) %all-reduce.8.cloned.1.call-update) | async-done | bytes 393232 | tf_op jit(solution)/shard_map/while/body/eval_jaxpr/psum | solution.py:13
  644.8 7.5 subtract_select_fusion.2
  654.2 4.8 select_n.633
  661.7 86.4 %all-reduce.4.cloned.1.call-done = f32[1536,128]{1,0:T(8,128)} async-done(((f32[1536,128]{1,0:T(8,128)}), f32[1536,128]{1,0:T(8,128)}) %all-reduce.4.cloned.1.call-update) | async-done | bytes 786448 | tf_op jit(solution)/shard_map/while/body/eval_jaxpr/psum | solution.py:13
  749.7 58.6 %all-reduce.6.cloned.1.call-done = f32[128,128]{1,0:T(8,128)} async-done(((f32[128,128]{1,0:T(8,128)}), f32[128,128]{1,0:T(8,128)}) %all-reduce.6.cloned.1.call-update) | async-done | bytes 65552 | tf_op jit(solution)/shard_map/while/body/eval_jaxpr/psum | solution.py:13
  810.2 11.7 %cholesky.80 = f32[128,128]{1,0:T(8,128)S(1)} custom-call(f32[128,128]{1,0:T(8,128)S(1)} %fusion.54), custom_call_target="Cholesky" | custom-call | tf_op jit(solution)/shard_map/while/body/eval_jaxpr/jit(cholesky)/cholesky | solution.py:124
  823.2 9.8 %custom-call.31 = f32[1,128,128]{1,2,0:T(8,128)S(1)} custom-call(f32[1,128,128]{2,1,0:T(8,128)S(1)} %select_bitcast_fusion.4), custom_call_target="InvertDiagBlocksLowerTriangular" | custom-call | tf_op jit(solution)/shard_map/while/body/eval_jaxpr/triangular_solve | solution.py:125
  836.9 59.4 %all-reduce.8.cloned.1.call-done = f32[768,128]{1,0:T(8,128)} async-done(((f32[768,128]{1,0:T(8,128)}), f32[768,128]{1,0:T(8,128)}) %all-reduce.8.cloned.1.call-update) | async-done | bytes 393232 | tf_op jit(solution)/shard_map/while/body/eval_jaxpr/psum | solution.py:13
  896.3 7.5 subtract_select_fusion.2
  905.7 4.7 select_n.633
  910.5 5.1 and_select_fusion
  (95 shorter events, 47.4 us)
Async XLA Ops:
  10.7 26.1 %all-to-all-start.1 = ((s32[8,1,2]{2,1,0:T(1,128)}), s32[8,1,2]{2,1,0:T(1,128)S(1)}, u32[]{:S(2)}, u32[]{:S(2)}) async-start(s32[8,1,2]{2,1,0:T(1,128)} %copy.50), calls=%async_computation.1 | async-start | bytes 8192 | tf_op jit(solution)/shard_map/all_to_all | solution.py:77
  36.8 99.7 %all-to-all-start.2 = ((f32[8,2,128,1024]{3,2,1,0:T(8,128)}), f32[8,2,128,1024]{3,2,1,0:T(8,128)}, u32[]{:S(2)}, u32[]{:S(2)}) async-start(f32[8,2,128,1024]{3,2,1,0:T(8,128)} %broadcast_select_fusion.1), calls=%async_computation.2 | async-start | bytes 16777216 | tf_op jit(solution)/shard_map/all_to_all | solution.py:76
  136.4 41.7 %all-to-all-start = ((s32[1,16,1]{2,0,1:T(1,128)}), s32[1,16,1]{2,0,1:T(1,128)S(1)}, u32[]{:S(2)}, u32[]{:S(2)}) async-start(s32[1,16,1]{2,0,1:T(1,128)} %copy.49), calls=%async_computation | async-start | bytes 16384 | tf_op jit(solution)/shard_map/all_to_all | solution.py:97
  178.1 190.7 %all-to-all-start.3 = ((f32[1536,16,1,128]{3,0,2,1:T(8,128)}), f32[1536,16,1,128]{3,0,2,1:T(8,128)}, u32[]{:S(2)}, u32[]{:S(2)}) async-start(f32[1536,16,1,128]{3,0,2,1:T(8,128)} %fusion.13), calls=%async_computation.3 | async-start | bytes 25165824 | tf_op jit(solution)/shard_map/all_to_all | solution.py:96
  407.4 88.9 %all-reduce.4.cloned.1.call-start = ((), (), s32[]{:S(2)}) async-start(), calls=%async_computation.4 | async-start | bytes 1572864 | tf_op jit(solution)/shard_map/while/body/eval_jaxpr/psum | solution.py:13
  410.0 146.8 %all-reduce.6.cloned.1.call-start = ((), (), s32[]{:S(2)}) async-start(), calls=%async_computation.5 | async-start | bytes 131072 | tf_op jit(solution)/shard_map/while/body/eval_jaxpr/psum | solution.py:13
  497.9 146.8 %all-reduce.8.cloned.1.call-start = ((), (), s32[]{:S(2)}) async-start(), calls=%async_computation.6 | async-start | bytes 786432 | tf_op jit(solution)/shard_map/while/body/eval_jaxpr/psum | solution.py:13
  659.0 89.1 %all-reduce.4.cloned.1.call-start = ((), (), s32[]{:S(2)}) async-start(), calls=%async_computation.4 | async-start | bytes 1572864 | tf_op jit(solution)/shard_map/while/body/eval_jaxpr/psum | solution.py:13
  661.6 146.8 %all-reduce.6.cloned.1.call-start = ((), (), s32[]{:S(2)}) async-start(), calls=%async_computation.5 | async-start | bytes 131072 | tf_op jit(solution)/shard_map/while/body/eval_jaxpr/psum | solution.py:13
  749.6 146.7 %all-reduce.8.cloned.1.call-start = ((), (), s32[]{:S(2)}) async-start(), calls=%async_computation.6 | async-start | bytes 786432 | tf_op jit(solution)/shard_map/while/body/eval_jaxpr/psum | solution.py:13
Sparse Core Ops, SparseCore 0:
  411.5 84.8 all-reduce.3
  498.8 58.0 all-reduce.5
  585.4 59.3 all-reduce.7
  662.7 85.2 all-reduce.3
  750.3 58.0 all-reduce.5
  836.9 59.3 all-reduce.7
where the time goes:
time: 924 us; the launch traced here: 922 us
  waiting for transfers between devices  678 us (73%)
  other arithmetic  109 us (12%)
  local copies, waits for them, and re-layouts  58.3 us (6%)
  matrix products  38.6 us (4%)
  starting transfers between devices  24.9 us (3%)
  between operations  13.5 us (1%)
    psum x6, waiting for transfers between devices, broadcast(): return lax.psum(kept, axis)  409 us
    all_to_all x1, waiting for transfers between devices, shards(): lax.all_to_all(outgoing_cols, 'col', split_axis=1, concat_axis=1, tiled=T...  177 us
    all_to_all x1, waiting for transfers between devices, shards(): lax.all_to_all(outgoing, 'row', split_axis=0, concat_axis=0, tiled=True)  92 us
    another operation x6, other arithmetic, finish(): factor = jnp.linalg.cholesky(corner)  24.8 us
    another operation x4, other arithmetic, finish(): lax.linalg.triangular_solve(factor, raw_panel, left_side=False, lower=Tru...  20.9 us
    dot_general x1, matrix products, shards(): jnp.einsum('rsb,su->rub', arrived_cols.reshape(local_rows, -1, B), landin...  19.7 us
  transfers between devices with their start and end apart: 10, of which 8 were waited for; matrix products, arithmetic and copies ran while one was open for 7% of the time, Pallas kernels for 0%

commit v1 on v0

--- a/solution.py
+++ b/solution.py
@@ -10,7 +10,7 @@
 
 def broadcast(value, axis, source):
     kept = jnp.where(lax.axis_index(axis) == source, value, 0).astype(value.dtype)
-    return lax.psum(kept, axis)
+    return jnp.sum(lax.all_gather(kept, axis), axis=0)
 
 
 def plan_slots(targets, usable, block_size, dest_count, slot_count):

time: 924 us -> 782 us (0.85)
  waiting for transfers between devices: 678 us -> 502 us
  blocking collectives: 0 us -> 26.9 us
  other arithmetic: 109 us -> 119 us
    psum x6 -> x0, waiting for transfers between devices: 409 us -> none  [broadcast(): return lax.psum(kept, axis)]
    all_gather x0 -> x4, waiting for transfers between devices: none -> 233 us  [broadcast(): return jnp.sum(lax.all_gather(kept, axis), axis=0)]
    all_gather x0 -> x2, blocking collectives: none -> 26.9 us  [broadcast(): return jnp.sum(lax.all_gather(kept, axis), axis=0)]
    reduce_sum x0 -> x6, other arithmetic: none -> 14.7 us  [broadcast(): return jnp.sum(lax.all_gather(kept, axis), axis=0)]
    another operation x6 -> x4, other arithmetic: 24.8 us -> 23.5 us  [finish(): factor = jnp.linalg.cholesky(corner)]
  transfers between devices with their start and end apart: 10 -> 8, of which waited for: 8 -> 6; matrix products, arithmetic and copies ran while one was open for 7% -> 8% of each run, Pallas kernels for 0% -> 0%
where the time goes in v1:
time: 782 us; the launch traced here: 779 us
  waiting for transfers between devices  502 us (64%)
  other arithmetic  119 us (15%)
  local copies, waits for them, and re-layouts  56.7 us (7%)
  matrix products  36.3 us (5%)
  blocking collectives  26.9 us (3%)
  starting transfers between devices  24.8 us (3%)
  between operations  13.2 us (2%)
    all_gather x4, waiting for transfers between devices, broadcast(): return jnp.sum(lax.all_gather(kept, axis), axis=0)  233 us
    all_to_all x1, waiting for transfers between devices, shards(): lax.all_to_all(outgoing_cols, 'col', split_axis=1, concat_axis=1, tiled=T...  177 us
    all_to_all x1, waiting for transfers between devices, shards(): lax.all_to_all(outgoing, 'row', split_axis=0, concat_axis=0, tiled=True)  92 us
    all_gather x2, blocking collectives, broadcast(): return jnp.sum(lax.all_gather(kept, axis), axis=0)  26.9 us
    another operation x4, other arithmetic, finish(): factor = jnp.linalg.cholesky(corner)  23.5 us
    another operation x4, other arithmetic, finish(): lax.linalg.triangular_solve(factor, raw_panel, left_side=False, lower=Tru...  20.9 us
    dot_general x1, matrix products, shards(): jnp.einsum('rsb,su->rub', arrived_cols.reshape(local_rows, -1, B), landin...  19.7 us
    unnamed x3, local copies, waits for them, and re-layouts  16.4 us
  transfers between devices with their start and end apart: 8, of which 6 were waited for; matrix products, arithmetic and copies ran while one was open for 8% of the time, Pallas kernels for 0%

profile of v1, /device:TPU:0, one launch (start us, length us, event | category | flops | bytes accessed | tf_op | source)
XLA Modules:
  0.0 779.1 jit_solution(1817419076585840823)
XLA Ops:
  21.7 6.5 gather_fusion
  28.1 8.6 %broadcast_select_fusion.1 = f32[8,2,128,1024]{3,2,1,0:T(8,128)} fusion(f32[8,2,128,1024]{3,2,1,0:T(8,128)} %bitcast.85, pred[8,2]{1,0:T(8,128)(4,1)S(1)} %copy.51), kind=kLoop, calls=%fused_computation.39 | loop fusion | flops 2097152 | bytes 16777232 | tf_op jit(solution)/shard_map/jit(_where)/select_n | solution.py:74
  36.8 5.0 all-to-all-start.2
  44.4 92.0 %all-to-all-done.2 = f32[8,2,128,1024]{3,2,1,0:T(8,128)} async-done(((f32[8,2,128,1024]{3,2,1,0:T(8,128)}), f32[8,2,128,1024]{3,2,1,0:T(8,128)}, u32[]{:S(2)}, u32[]{:S(2)}) %all-to-all-start.2) | async-done | bytes 8388640 | tf_op jit(solution)/shard_map/all_to_all | solution.py:76
  136.4 7.9 %all-to-all-start = ((s32[1,16,1]{2,0,1:T(1,128)}), s32[1,16,1]{2,0,1:T(1,128)S(1)}, u32[]{:S(2)}, u32[]{:S(2)}) async-start(s32[1,16,1]{2,0,1:T(1,128)} %copy.49), calls=%async_computation | async-start | bytes 16384 | tf_op jit(solution)/shard_map/all_to_all | solution.py:97
  144.3 7.0 gather_fusion.1
  159.1 8.6 %gather_fusion.2 = f32[16,1536,128]{2,1,0:T(8,128)} fusion(f32[1536,8,128]{2,0,1:T(8,128)} %copy_select_fusion, s32[1024]{0:T(1024)S(1)} %pad_clamp_fusion), kind=kCustom, calls=%fused_computation.2 | custom fusion | bytes 25165888 | tf_op jit(solution)/shard_map/gather | solution.py:94
  167.7 10.4 %fusion.13 = f32[1536,16,1,128]{3,0,2,1:T(8,128)} fusion(f32[16,1536,128]{2,1,0:T(8,128)} %gather_fusion.2, pred[16]{0:T(512)(128)(4,1)S(1)} %fusion.32), kind=kLoop, calls=%fused_computation.32 | loop fusion | flops 3145728 | bytes 25165840 | tf_op jit(solution)/shard_map/jit(_where)/select_n | solution.py:94
  178.1 7.3 all-to-all-start.3
  185.4 6.0 copy.57
  191.8 176.9 %all-to-all-done.3 = f32[1536,16,1,128]{3,0,2,1:T(8,128)} async-done(((f32[1536,16,1,128]{3,0,2,1:T(8,128)}), f32[1536,16,1,128]{3,0,2,1:T(8,128)}, u32[]{:S(2)}, u32[]{:S(2)}) %all-to-all-start.3) | async-done | bytes 12582944 | tf_op jit(solution)/shard_map/all_to_all | solution.py:96
  368.8 19.7 %fusion.17 = f32[1536,6,128]{2,1,0:T(8,128)} fusion(f32[1536,16,1,128]{3,0,2,1:T(8,128)} %all-to-all-done.3, s32[16]{0:T(128)S(1)} %reduce.25), kind=kOutput, calls=%fused_computation.41 | convolution fusion | flops 226492512 | bytes 17301568 | tf_op jit(solution)/shard_map/rsb,su->rub/dot_general | solution.py:102
  388.4 6.0 copy.56
  394.5 6.9 bitcast_add_fusion.1
  401.4 6.0 copy.58
  407.5 360.0 %while.18 = (s32[]{:T(128)}, f32[1536,768]{1,0:T(8,128)}, s32[]{:T(128)}, s32[]{:T(128)}, s32[]{:T(128)}, /*index=5*/s32[]{:T(128)}, s32[]{:T(128)}, s32[]{:T(12...) while((s32[]{:T(128)}, f32[1536,768]{1,0:T(8,128)}, ...), condition=%wide.region_20.21_spmd.clone.clone, body=%wide.region_14.20_spmd.clone.clone.sunk | while | flops 2122346240 | bytes 89803736 | solution.py:171
  410.2 89.1 %all-gather.18.cloned.1.call-done = f32[24576,128]{1,0:T(8,128)} async-done(((f32[1536,128]{1,0:T(8,128)}), f32[24576,128]{1,0:T(8,128)}) %all-gather.18.cloned.1.call-update) | async-done | bytes 12582928 | tf_op jit(solution)/shard_map/while/body/eval_jaxpr/all_gather | solution.py:13
  499.3 5.2 reduce_sum.202
  504.5 13.4 %all-gather.13 = f32[1024,128]{1,0:T(8,128)S(1)} all-gather(f32[128,128]{1,0:T(8,128)S(1)} %dynamic-slice_select_fusion.9), channel_id=3, replica_groups=mesh['col'=16,'row'=8] {'row'}, dimensions={0}, use_global_device_ids=true | all-gather | bytes 589824 | tf_op jit(solution)/shard_map/while/body/eval_jaxpr/all_gather | solution.py:13
  518.1 11.7 %cholesky.76 = f32[128,128]{1,0:T(8,128)S(1)} custom-call(f32[128,128]{1,0:T(8,128)S(1)} %fusion.54), custom_call_target="Cholesky" | custom-call | tf_op jit(solution)/shard_map/while/body/eval_jaxpr/jit(cholesky)/cholesky | solution.py:124
  531.2 9.8 %custom-call.31 = f32[1,128,128]{1,2,0:T(8,128)S(1)} custom-call(f32[1,128,128]{2,1,0:T(8,128)S(1)} %select_bitcast_fusion.4), custom_call_target="InvertDiagBlocksLowerTriangular" | custom-call | tf_op jit(solution)/shard_map/while/body/eval_jaxpr/triangular_solve | solution.py:125
  543.7 26.8 %all-gather.20.cloned.1.call-done = f32[6144,128]{1,0:T(8,128)} async-done(((f32[768,128]{1,0:T(8,128)}), f32[6144,128]{1,0:T(8,128)}) %all-gather.20.cloned.1.call-update) | async-done | bytes 3145744 | tf_op jit(solution)/shard_map/while/body/eval_jaxpr/all_gather | solution.py:13
  572.6 7.5 subtract_select_fusion.2
  589.5 90.4 %all-gather.18.cloned.1.call-done = f32[24576,128]{1,0:T(8,128)} async-done(((f32[1536,128]{1,0:T(8,128)}), f32[24576,128]{1,0:T(8,128)}) %all-gather.18.cloned.1.call-update) | async-done | bytes 12582928 | tf_op jit(solution)/shard_map/while/body/eval_jaxpr/all_gather | solution.py:13
  679.9 5.2 reduce_sum.202
  685.2 13.4 %all-gather.13 = f32[1024,128]{1,0:T(8,128)S(1)} all-gather(f32[128,128]{1,0:T(8,128)S(1)} %dynamic-slice_select_fusion.9), channel_id=3, replica_groups=mesh['col'=16,'row'=8] {'row'}, dimensions={0}, use_global_device_ids=true | all-gather | bytes 589824 | tf_op jit(solution)/shard_map/while/body/eval_jaxpr/all_gather | solution.py:13
  698.8 11.7 %cholesky.76 = f32[128,128]{1,0:T(8,128)S(1)} custom-call(f32[128,128]{1,0:T(8,128)S(1)} %fusion.54), custom_call_target="Cholesky" | custom-call | tf_op jit(solution)/shard_map/while/body/eval_jaxpr/jit(cholesky)/cholesky | solution.py:124
  711.9 9.8 %custom-call.31 = f32[1,128,128]{1,2,0:T(8,128)S(1)} custom-call(f32[1,128,128]{2,1,0:T(8,128)S(1)} %select_bitcast_fusion.4), custom_call_target="InvertDiagBlocksLowerTriangular" | custom-call | tf_op jit(solution)/shard_map/while/body/eval_jaxpr/triangular_solve | solution.py:125
  724.4 26.8 %all-gather.20.cloned.1.call-done = f32[6144,128]{1,0:T(8,128)} async-done(((f32[768,128]{1,0:T(8,128)}), f32[6144,128]{1,0:T(8,128)}) %all-gather.20.cloned.1.call-update) | async-done | bytes 3145744 | tf_op jit(solution)/shard_map/while/body/eval_jaxpr/all_gather | solution.py:13
  753.3 7.5 subtract_select_fusion.2
  762.7 4.8 select_n.633
  767.5 5.1 and_select_fusion
  (95 shorter events, 52.1 us)
Async XLA Ops:
  10.7 26.1 %all-to-all-start.1 = ((s32[8,1,2]{2,1,0:T(1,128)}), s32[8,1,2]{2,1,0:T(1,128)S(1)}, u32[]{:S(2)}, u32[]{:S(2)}) async-start(s32[8,1,2]{2,1,0:T(1,128)} %copy.50), calls=%async_computation.1 | async-start | bytes 8192 | tf_op jit(solution)/shard_map/all_to_all | solution.py:77
  36.8 99.7 %all-to-all-start.2 = ((f32[8,2,128,1024]{3,2,1,0:T(8,128)}), f32[8,2,128,1024]{3,2,1,0:T(8,128)}, u32[]{:S(2)}, u32[]{:S(2)}) async-start(f32[8,2,128,1024]{3,2,1,0:T(8,128)} %broadcast_select_fusion.1), calls=%async_computation.2 | async-start | bytes 16777216 | tf_op jit(solution)/shard_map/all_to_all | solution.py:76
  136.4 41.7 %all-to-all-start = ((s32[1,16,1]{2,0,1:T(1,128)}), s32[1,16,1]{2,0,1:T(1,128)S(1)}, u32[]{:S(2)}, u32[]{:S(2)}) async-start(s32[1,16,1]{2,0,1:T(1,128)} %copy.49), calls=%async_computation | async-start | bytes 16384 | tf_op jit(solution)/shard_map/all_to_all | solution.py:97
  178.1 190.7 %all-to-all-start.3 = ((f32[1536,16,1,128]{3,0,2,1:T(8,128)}), f32[1536,16,1,128]{3,0,2,1:T(8,128)}, u32[]{:S(2)}, u32[]{:S(2)}) async-start(f32[1536,16,1,128]{3,0,2,1:T(8,128)} %fusion.13), calls=%async_computation.3 | async-start | bytes 25165824 | tf_op jit(solution)/shard_map/all_to_all | solution.py:96
  407.5 91.8 %all-gather.18.cloned.1.call-start = ((), (), s32[]{:S(2)}) async-start(), calls=%async_computation.4 | async-start | bytes 13369344 | tf_op jit(solution)/shard_map/while/body/eval_jaxpr/all_gather | solution.py:13
  410.0 160.5 %all-gather.20.cloned.1.call-start = ((), (), s32[]{:S(2)}) async-start(), calls=%async_computation.5 | async-start | bytes 3538944 | tf_op jit(solution)/shard_map/while/body/eval_jaxpr/all_gather | solution.py:13
  586.8 93.2 %all-gather.18.cloned.1.call-start = ((), (), s32[]{:S(2)}) async-start(), calls=%async_computation.4 | async-start | bytes 13369344 | tf_op jit(solution)/shard_map/while/body/eval_jaxpr/all_gather | solution.py:13
  589.4 161.8 %all-gather.20.cloned.1.call-start = ((), (), s32[]{:S(2)}) async-start(), calls=%async_computation.5 | async-start | bytes 3538944 | tf_op jit(solution)/shard_map/while/body/eval_jaxpr/all_gather | solution.py:13
Sparse Core Ops, SparseCore 0:
  410.4 88.8 all-gather.17
  543.7 26.7 all-gather.19
  589.8 90.1 all-gather.17
  724.4 26.7 all-gather.19
